TPU v7x, 32 devices: a whole 2x2x4 slice. The times are simulated.
32 devices in a mesh: parts: 2 (over y), space: 4 (over z), tm: 2 (over x), spin: 2 (over core).
Axes of the slice: x: 2, y: 2, z: 4, core: 2. Of those that a mesh axis runs over, the one named last changes fastest.
Arguments:
- backward: bfloat16 [4, 2, 4, 64, 3, 4, 128], P('parts', 'tm', None, 'spin', None, 'space'), parts along dimension 0, may hold values from -6 to 6
- forward: bfloat16 [4, 2, 4, 64, 3, 4, 128], P('parts', 'tm', None, 'spin', None, 'space'), parts along dimension 0, may hold values from -6 to 6
- gauge_links: bfloat16 [4, 3, 3, 3, 2, 4, 128], P('parts', None, None, None, 'tm', 'space'), parts along dimension 0, may hold values from -2.5 to 2.5
- momenta: int32 [3, 3], replicated, may hold values from -2 to 2
- gamma_list: int32 [16], replicated, may hold values from 0 to 15
Outputs:
- insertion: float32 [4, 3, 16, 2, 64, 64], P('parts', None, None, 'tm', 'space', 'spin'), parts along dimension 0
There are 2 independent parts, one for each index of `parts`. A program takes and returns all parts, laid end to end along the dimension named above; an argument that names none is the same for every part. Nothing has to cross between parts.
All inputs are finite; a program needn't handle non-finite values.
Results may differ from a plain program's by a relative error of at most 0.0056.
Values may be sent and summed in bfloat16 or wider, within the bound.
A program may use at most 64 MiB of HBM per device.

v0:
```python
import math

import jax
import jax.numpy as jnp
import numpy as np
from jax import lax
from jax.sharding import PartitionSpec as P

LX = 32


def passed_along(value, axis, steps):
    count = lax.axis_size(axis)
    pairs = [(source, (source + steps) % count) for source in range(count)]
    return lax.ppermute(value, axis, pairs)


def gamma_tables():
    zeros = np.zeros((4, 4))
    gx_imag = np.array([[0, 0, 0, 1], [0, 0, 1, 0], [0, -1, 0, 0], [-1, 0, 0, 0]]) * 1.0
    gy_real = np.array([[0, 0, 0, -1], [0, 0, 1, 0], [0, 1, 0, 0], [-1, 0, 0, 0]]) * 1.0
    gz_imag = np.array([[0, 0, 1, 0], [0, 0, 0, -1], [-1, 0, 0, 0], [0, 1, 0, 0]]) * 1.0
    gt_real = np.array([[0, 0, 1, 0], [0, 0, 0, 1], [1, 0, 0, 0], [0, 1, 0, 0]]) * 1.0
    singles = [(zeros, gx_imag), (gy_real, zeros), (zeros, gz_imag), (gt_real, zeros)]
    clif_real = []
    clif_imag = []
    for number in range(16):
        mat_real = np.eye(4)
        mat_imag = np.zeros((4, 4))
        for which in range(4):
            if number >> which & 1:
                other_real, other_imag = singles[which]
                new_real = mat_real @ other_real - mat_imag @ other_imag
                new_imag = mat_real @ other_imag + mat_imag @ other_real
                mat_real, mat_imag = (new_real, new_imag)
        clif_real.append(mat_real)
        clif_imag.append(mat_imag)
    return (singles, (np.stack(clif_real), np.stack(clif_imag)))


def chosen_gammas(gamma_list):
    singles, clifford = gamma_tables()
    table_real = jnp.asarray(clifford[0], dtype=jnp.float32)
    table_imag = jnp.asarray(clifford[1], dtype=jnp.float32)
    one_hot = (gamma_list[:, None] == jnp.arange(16, dtype=jnp.int32)[None, :]).astype(jnp.float32)
    gam_real = jnp.einsum("kg,gsv->ksv", one_hot, table_real, precision=lax.Precision.HIGHEST)
    gam_imag = jnp.einsum("kg,gsv->ksv", one_hot, table_imag, precision=lax.Precision.HIGHEST)
    return (gam_real, gam_imag)


def color_apply(link_real, link_imag, spin_real, spin_imag, dagger):
    outs_real = []
    outs_imag = []
    for c in range(3):
        summed_real = 0.0
        summed_imag = 0.0
        for d in range(3):
            if dagger:
                coef_real = link_real[d, c]
                coef_imag = -link_imag[d, c]
            else:
                coef_real = link_real[c, d]
                coef_imag = link_imag[c, d]
            coef_real = coef_real[..., None, None, :, :]
            coef_imag = coef_imag[..., None, None, :, :]
            part_real = spin_real[..., d, :, :]
            part_imag = spin_imag[..., d, :, :]
            summed_real = summed_real + coef_real * part_real - coef_imag * part_imag
            summed_imag = summed_imag + coef_real * part_imag + coef_imag * part_real
        outs_real.append(summed_real)
        outs_imag.append(summed_imag)
    return (jnp.stack(outs_real, axis=-3), jnp.stack(outs_imag, axis=-3))


def spin_apply(matrix, spin_real, spin_imag):
    outs_real = []
    outs_imag = []
    for t in range(4):
        summed_real = 0.0
        summed_imag = 0.0
        for s in range(4):
            coef_real = float(matrix[0][t, s])
            coef_imag = float(matrix[1][t, s])
            if coef_real == 0.0 and coef_imag == 0.0:
                continue
            part_real = spin_real[..., s, :, :, :, :]
            part_imag = spin_imag[..., s, :, :, :, :]
            summed_real = summed_real + coef_real * part_real - coef_imag * part_imag
            summed_imag = summed_imag + coef_real * part_imag + coef_imag * part_real
        outs_real.append(summed_real)
        outs_imag.append(summed_imag)
    return (jnp.stack(outs_real, axis=-5), jnp.stack(outs_imag, axis=-5))


def plane_roll(spinor, offset, along_y, width_x):
    initial = spinor.shape
    gridded = spinor.reshape(initial[:-1] + (initial[-1] // width_x, width_x))
    gridded = jnp.roll(gridded, offset, axis=-2 if along_y else -1)
    return gridded.reshape(initial)


def current(fwd_real, fwd_imag, link_real, link_imag, up_z, down_z, width_x):
    singles, clifford = gamma_tables()
    summed_real = 0.0
    summed_imag = 0.0
    for direction in range(3):
        single_real, single_imag = singles[direction]
        minus_proj = ((np.eye(4) - single_real) / 2.0, -single_imag / 2.0)
        plus_proj = ((np.eye(4) + single_real) / 2.0, single_imag / 2.0)
        if direction < 2:
            along_y = direction == 1
            up_real = plane_roll(fwd_real, -1, along_y, width_x)
            up_imag = plane_roll(fwd_imag, -1, along_y, width_x)
            back_real, back_imag = color_apply(
                link_real[direction], link_imag[direction], fwd_real, fwd_imag, True
            )
            down_real = plane_roll(back_real, 1, along_y, width_x)
            down_imag = plane_roll(back_imag, 1, along_y, width_x)
        else:
            up_real, up_imag = up_z
            down_real, down_imag = down_z
        hop_real, hop_imag = color_apply(
            link_real[direction], link_imag[direction], up_real, up_imag, False
        )
        ahead_real, ahead_imag = spin_apply(minus_proj, hop_real, hop_imag)
        behind_real, behind_imag = spin_apply(plus_proj, down_real, down_imag)
        summed_real = summed_real + ahead_real - behind_real
        summed_imag = summed_imag + ahead_imag - behind_imag
    return (summed_real, summed_imag)


def phase_list(momenta, z_start, layers, plane_size, width_x, width_y, full_z):
    sites = jnp.arange(plane_size, dtype=jnp.int32)
    coord_x = sites % width_x
    coord_y = sites // width_x
    coord_z = z_start + jnp.arange(layers, dtype=jnp.int32)
    result = []
    for number in range(momenta.shape[0]):
        frac_plane = jnp.mod(momenta[number, 0] * coord_x, width_x).astype(jnp.float32) / float(
            width_x
        )
        frac_plane = frac_plane + jnp.mod(momenta[number, 1] * coord_y, width_y).astype(
            jnp.float32
        ) / float(width_y)
        frac_depth = jnp.mod(momenta[number, 2] * coord_z, full_z).astype(jnp.float32) / float(
            full_z
        )
        result.append(2.0 * math.pi * (frac_depth[:, None] + frac_plane[None, :]))
    return result


def contract(back_piece, weave_re, weave_im, thetas, gam_real, gam_imag, scaling):
    back_real = back_piece[0].astype(jnp.float32)
    back_imag = back_piece[1].astype(jnp.float32)
    slab_times, spins, columns = (back_real.shape[0], back_real.shape[1], back_real.shape[2])
    blocks = []
    for theta in thetas:
        cosine = jnp.cos(theta)
        sine_part = jnp.sin(theta)
        rot_real = (cosine * back_real - sine_part * back_imag).astype(jnp.bfloat16)
        rot_imag = (sine_part * back_real + cosine * back_imag).astype(jnp.bfloat16)
        stacked = jnp.concatenate(
            [
                rot_real.reshape(slab_times, spins, columns, -1),
                rot_imag.reshape(slab_times, spins, columns, -1),
            ],
            axis=-1,
        )
        pair_real = jnp.einsum(
            "usak,uvbk->usvab", stacked, weave_re, preferred_element_type=jnp.float32
        )
        pair_imag = jnp.einsum(
            "usak,uvbk->usvab", stacked, weave_im, preferred_element_type=jnp.float32
        )
        out_real = jnp.einsum(
            "ksv,usvab->kuab", gam_real, pair_real, precision=lax.Precision.HIGHEST
        ) - jnp.einsum("ksv,usvab->kuab", gam_imag, pair_imag, precision=lax.Precision.HIGHEST)
        out_imag = jnp.einsum(
            "ksv,usvab->kuab", gam_real, pair_imag, precision=lax.Precision.HIGHEST
        ) + jnp.einsum("ksv,usvab->kuab", gam_imag, pair_real, precision=lax.Precision.HIGHEST)
        blocks.append(jnp.stack([out_real, out_imag]) * scaling)
    return jnp.stack(blocks, axis=1)


def body(backward, forward, gauge_links, momenta, gamma_list):
    layers = forward.shape[5]
    plane_size = forward.shape[6]
    width_x = LX
    full_z = layers * lax.axis_size("space")
    z_start = lax.axis_index("space") * layers
    fwd_real = forward[0].astype(jnp.float32)
    fwd_imag = forward[1].astype(jnp.float32)
    link_real = gauge_links[0].astype(jnp.float32)
    link_imag = gauge_links[1].astype(jnp.float32)
    back_real, back_imag = color_apply(link_real[2], link_imag[2], fwd_real, fwd_imag, True)
    hopped = jnp.stack([back_real, back_imag])
    carried = passed_along(hopped[:, :, :, :, :, -1:, :], "space", 1)
    down_both = jnp.concatenate([carried, hopped[:, :, :, :, :, :-1, :]], axis=5)
    down_z = (down_both[0], down_both[1])
    following = passed_along(forward[:, :, :, :, :, :1, :], "space", -1)
    up_both = jnp.concatenate([forward[:, :, :, :, :, 1:, :], following], axis=5).astype(
        jnp.float32
    )
    up_z = (up_both[0], up_both[1])
    weave_real, weave_imag = current(
        fwd_real, fwd_imag, link_real, link_imag, up_z, down_z, width_x
    )
    slab_times = forward.shape[1]
    flat_real = weave_real.astype(jnp.bfloat16).reshape(slab_times, 4, forward.shape[3], -1)
    flat_imag = weave_imag.astype(jnp.bfloat16).reshape(slab_times, 4, forward.shape[3], -1)
    weave_re = jnp.concatenate([flat_real, flat_imag], axis=-1)
    weave_im = jnp.concatenate([flat_imag, -flat_real], axis=-1)
    thetas = phase_list(
        momenta, z_start, layers, plane_size, width_x, plane_size // width_x, full_z
    )
    gam_real, gam_imag = chosen_gammas(gamma_list)
    scaling = 1.0 / math.sqrt(3.0 * plane_size * full_z)
    partial_value = contract(
        lax.all_gather(backward, "spin", axis=3, tiled=True),
        weave_re,
        weave_im,
        thetas,
        gam_real,
        gam_imag,
        scaling,
    )
    return lax.psum_scatter(partial_value, "space", scatter_dimension=4, tiled=True)


def solution(mesh):
    in_specs = (
        P("parts", "tm", None, "spin", None, "space", None),
        P("parts", "tm", None, "spin", None, "space", None),
        P("parts", None, None, None, "tm", "space", None),
        P(),
        P(),
    )
    out_specs = P("parts", None, None, "tm", "space", "spin")
    return jax.shard_map(body, mesh=mesh, in_specs=in_specs, out_specs=out_specs, check_vma=False)
```

profile of v0, /device:TPU:0, one launch (start us, length us, event | category | flops | bytes accessed | tf_op | source)
XLA Modules:
  0.0 148.8 jit_solution(2458205223803730476)
XLA Ops:
  6.5 5.1 %collective-permute-start = (bf16[2,1,4,32,3,1,128]{6,3,4,2,5,1,0:T(8,128)(2,1)}, bf16[2,1,4,32,3,1,128]{6,3,4,2,5,1,0:T(8,128)(2,1)}, u32[]{:S(2)}, u32[]{:S(2)}) collective-permute-start(bf16[2,1,4,32,3,1,128]{6,3,4,2,5,1,0:T(8,128)(2,1)} %bitcast.720), channel_id=1, source_target_pairs={{0,12},{4,0},{8,4},{12,8},{1,13},{5,1},{9,5},{13,9},{2,14},{6,2},{... | collective-permute-start | bytes 589832 | tf_op jit(solution)/shard_map/ppermute | solution.py:15
  11.6 1.0 fusion.43
  12.6 0.9 fusion.42
  13.5 0.8 slice_convert_fusion.5
  15.7 0.8 pad_maximum_fusion.9
  20.9 0.7 add_subtract_fusion.5
  21.6 0.7 add_subtract_fusion.4
  22.8 0.8 slice.939
  24.2 0.8 slice.934
  25.0 1.3 pad_maximum_fusion.6
  26.3 2.2 %reshape.3442 = f32[1,4,32,3,1,128]{5,2,3,1,4,0:T(8,128)} reshape(f32[1,4,32,3,1,4,32]{6,5,2,3,1,4,0:T(4,128)} %pad_maximum_fusion.6) | data formatting | bytes 393216 | tf_op jit(solution)/shard_map/reshape | solution.py:99
  28.5 1.4 pad_maximum_fusion.5
  30.3 1.0 multiply_subtract_fusion.11
  31.3 0.8 multiply_subtract_fusion.10
  32.2 0.7 add_subtract_fusion.7
  32.9 0.7 multiply_subtract_fusion.23
  34.3 0.7 multiply_subtract_fusion.14
  35.2 0.7 multiply_subtract_fusion.13
  36.0 0.7 multiply_subtract_fusion.12
  40.4 0.7 add_subtract_fusion.11
  41.1 0.7 add_subtract_fusion.10
  45.6 0.7 fusion.83
  50.8 1.4 fusion.75
  52.3 1.4 fusion.77
  53.7 1.3 fusion.79
  55.0 2.1 %all_gather.3 = bf16[2,1,4,64,3,1,128]{6,3,5,4,2,1,0:T(8,128)(2,1)S(1)} all-gather(bf16[2,1,4,32,3,1,128]{6,3,5,4,2,1,0:T(8,128)(2,1)S(1)} %copy-done.23), channel_id=1, replica_groups=mesh['parts'=2,'space'=4,'tm'=2,'spin'=2] {'spin'}, dimensions={3}, use_global_device_ids=true | all-gather | bytes 589824 | tf_op jit(solution)/shard_map/all_gather | solution.py:219
  58.5 1.1 subtract_convert_fusion.2
  59.9 1.0 convert_element_type.352
  62.1 1.0 slice_bitcast_fusion
  74.7 2.8 %copy.202 = f32[2,3,16,1,64,32]{5,2,3,1,0,4:T(8,128)} copy(f32[2,3,16,1,64,32]{4,2,5,3,1,0:T(8,128)S(1)} %pad_maximum_fusion) | data formatting | bytes 1572864 | tf_op jit(solution)/shard_map/stack | solution.py:182
  77.5 62.0 %reduce-scatter.2.cloned.1.call-done = f32[2,3,16,1,16,32]{5,2,3,1,0,4:T(8,128)} async-done(((f32[2,3,16,1,64,32]{5,2,3,1,0,4:T(8,128)}), f32[2,3,16,1,16,32]{5,2,3,1,0,4:T(8,128)}) %reduce-scatter.2.cloned.1.call-update) | async-done | bytes 196624 | tf_op jit(solution)/shard_map/reduce_scatter | solution.py:227
  139.5 2.5 %copy.203 = f32[2,3,16,1,16,32]{5,4,3,2,1,0:T(8,128)} copy(f32[2,3,16,1,16,32]{5,2,3,1,0,4:T(8,128)} %reduce-scatter.2.cloned.1.call-done) | data formatting | bytes 393216 | tf_op jit(solution)/shard_map/reduce_scatter | solution.py:227
  (406 shorter events, 30.4 us)
Async XLA Ops:
  6.5 133.0 %reduce-scatter.2.cloned.1.call-start = ((), (), s32[]{:S(2)}) async-start(), calls=%async_computation.1 | async-start | bytes 3932160 | tf_op jit(solution)/shard_map/reduce_scatter | solution.py:227
  6.5 53.3 %collective-permute-start = (bf16[2,1,4,32,3,1,128]{6,3,4,2,5,1,0:T(8,128)(2,1)}, bf16[2,1,4,32,3,1,128]{6,3,4,2,5,1,0:T(8,128)(2,1)}, u32[]{:S(2)}, u32[]{:S(2)}) collective-permute-start(bf16[2,1,4,32,3,1,128]{6,3,4,2,5,1,0:T(8,128)(2,1)} %bitcast.720), channel_id=1, source_target_pairs={{0,12},{4,0},{8,4},{12,8},{1,13},{5,1},{9,5},{13,9},{2,14},{6,2},{... | collective-permute-start | bytes 589832 | tf_op jit(solution)/shard_map/ppermute | solution.py:15
  16.5 45.6 %collective-permute-start.1 = (f32[2,1,4,32,3,1,128]{6,3,4,2,5,1,0:T(8,128)}, f32[2,1,4,32,3,1,128]{6,3,4,2,5,1,0:T(8,128)}, u32[]{:S(2)}, u32[]{:S(2)}) collective-permute-start(f32[2,1,4,32,3,1,128]{6,3,4,2,5,1,0:T(8,128)} %pad_maximum_fusion.9), channel_id=1, source_target_pairs={{0,4},{4,8},{8,12},{12,0},{1,5},{5,9},{9,13},{13,1},{2,6},{6,10},{... | collective-permute-start | bytes 1179656 | tf_op jit(solution)/shard_map/ppermute | solution.py:15
  34.2 2.7 %copy-start.58 = (f32[128]{0:T(128)}, f32[128]{0:T(128)S(1)}, u32[]{:S(2)}) copy-start(f32[128]{0:T(128)S(1)} %get-tuple-element.191) | copy-start | bytes 1540
  34.2 2.7 %copy-start.60 = (f32[128]{0:T(128)}, f32[128]{0:T(128)S(1)}, u32[]{:S(2)}) copy-start(f32[128]{0:T(128)S(1)} %get-tuple-element.192) | copy-start | bytes 1540
  34.2 2.7 %copy-start.62 = (f32[128]{0:T(128)}, f32[128]{0:T(128)S(1)}, u32[]{:S(2)}) copy-start(f32[128]{0:T(128)S(1)} %get-tuple-element.193) | copy-start | bytes 1540
  34.2 2.7 %copy-start.67 = (f32[128]{0:T(128)}, f32[128]{0:T(128)S(1)}, u32[]{:S(2)}) copy-start(f32[128]{0:T(128)S(1)} %get-tuple-element.187) | copy-start | bytes 1540
  34.3 2.7 %copy-start.69 = (f32[128]{0:T(128)}, f32[128]{0:T(128)S(1)}, u32[]{:S(2)}) copy-start(f32[128]{0:T(128)S(1)} %get-tuple-element.194) | copy-start | bytes 1540
  34.3 2.7 %copy-start.71 = (f32[128]{0:T(128)}, f32[128]{0:T(128)S(1)}, u32[]{:S(2)}) copy-start(f32[128]{0:T(128)S(1)} %get-tuple-element.195) | copy-start | bytes 1540
  44.9 3.3 %copy-start.9 = (f32[1,1,32,3,1,128]{5,2,3,1,4,0:T(8,128)S(1)}, f32[1,1,32,3,1,128]{5,2,3,1,4,0:T(8,128)}, u32[]{:S(2)}) copy-start(f32[1,1,32,3,1,128]{5,2,3,1,4,0:T(8,128)} %get-tuple-element.75) | copy-start | bytes 147460
  45.0 3.3 %copy-start.7 = (f32[1,1,32,3,1,128]{5,2,3,1,4,0:T(8,128)S(1)}, f32[1,1,32,3,1,128]{5,2,3,1,4,0:T(8,128)}, u32[]{:S(2)}) copy-start(f32[1,1,32,3,1,128]{5,2,3,1,4,0:T(8,128)} %get-tuple-element.78) | copy-start | bytes 147460
  45.1 3.4 %copy-start.25 = (f32[1,1,32,3,1,128]{5,2,3,1,4,0:T(8,128)S(1)}, f32[1,1,32,3,1,128]{5,2,3,1,4,0:T(8,128)}, u32[]{:S(2)}) copy-start(f32[1,1,32,3,1,128]{5,2,3,1,4,0:T(8,128)} %get-tuple-element.79) | copy-start | bytes 147460
  45.1 3.4 %copy-start.14 = (f32[1,1,32,3,1,128]{5,2,3,1,4,0:T(8,128)S(1)}, f32[1,1,32,3,1,128]{5,2,3,1,4,0:T(8,128)}, u32[]{:S(2)}) copy-start(f32[1,1,32,3,1,128]{5,2,3,1,4,0:T(8,128)} %get-tuple-element.69) | copy-start | bytes 147460
  45.2 3.4 %copy-start.12 = (f32[1,1,32,3,1,128]{5,2,3,1,4,0:T(8,128)S(1)}, f32[1,1,32,3,1,128]{5,2,3,1,4,0:T(8,128)}, u32[]{:S(2)}) copy-start(f32[1,1,32,3,1,128]{5,2,3,1,4,0:T(8,128)} %get-tuple-element.71) | copy-start | bytes 147460
  45.2 3.5 %copy-start.13 = (f32[1,1,32,3,1,128]{5,2,3,1,4,0:T(8,128)S(1)}, f32[1,1,32,3,1,128]{5,2,3,1,4,0:T(8,128)}, u32[]{:S(2)}) copy-start(f32[1,1,32,3,1,128]{5,2,3,1,4,0:T(8,128)} %get-tuple-element.73) | copy-start | bytes 147460
  45.3 3.6 %copy-start.22 = (f32[1,1,32,3,1,128]{5,2,3,1,4,0:T(8,128)S(1)}, f32[1,1,32,3,1,128]{5,2,3,1,4,0:T(8,128)}, u32[]{:S(2)}) copy-start(f32[1,1,32,3,1,128]{5,2,3,1,4,0:T(8,128)} %get-tuple-element.61) | copy-start | bytes 147460
  45.3 3.7 %copy-start.20 = (f32[1,1,32,3,1,128]{5,2,3,1,4,0:T(8,128)S(1)}, f32[1,1,32,3,1,128]{5,2,3,1,4,0:T(8,128)}, u32[]{:S(2)}) copy-start(f32[1,1,32,3,1,128]{5,2,3,1,4,0:T(8,128)} %get-tuple-element.64) | copy-start | bytes 147460
  45.3 3.7 %copy-start.21 = (f32[1,1,32,3,1,128]{5,2,3,1,4,0:T(8,128)S(1)}, f32[1,1,32,3,1,128]{5,2,3,1,4,0:T(8,128)}, u32[]{:S(2)}) copy-start(f32[1,1,32,3,1,128]{5,2,3,1,4,0:T(8,128)} %get-tuple-element.65) | copy-start | bytes 147460
  45.3 3.8 %copy-start.19 = (f32[1,1,32,3,1,128]{5,2,3,1,4,0:T(8,128)S(1)}, f32[1,1,32,3,1,128]{5,2,3,1,4,0:T(8,128)}, u32[]{:S(2)}) copy-start(f32[1,1,32,3,1,128]{5,2,3,1,4,0:T(8,128)} %get-tuple-element.66) | copy-start | bytes 147460
  49.7 5.4 %copy-start.23 = (bf16[2,1,4,32,3,1,128]{6,3,5,4,2,1,0:T(8,128)(2,1)S(1)}, bf16[2,1,4,32,3,1,128]{6,3,5,4,2,1,0:T(8,128)(2,1)}, u32[]{:S(2)}) copy-start(bf16[2,1,4,32,3,1,128]{6,3,5,4,2,1,0:T(8,128)(2,1)} %param.7) | copy-start | bytes 589828
  58.4 2.5 %copy-start.42 = (f32[128]{0:T(128)S(1)}, f32[128]{0:T(128)}, u32[]{:S(2)}) copy-start(f32[128]{0:T(128)} %copy-done.41) | copy-start | bytes 1540
  58.4 2.5 %copy-start.44 = (f32[128]{0:T(128)S(1)}, f32[128]{0:T(128)}, u32[]{:S(2)}) copy-start(f32[128]{0:T(128)} %copy-done.43) | copy-start | bytes 1540
  58.4 2.5 %copy-start.46 = (f32[128]{0:T(128)S(1)}, f32[128]{0:T(128)}, u32[]{:S(2)}) copy-start(f32[128]{0:T(128)} %copy-done.45) | copy-start | bytes 1540
  58.4 2.5 %copy-start.79 = (f32[128]{0:T(128)S(1)}, f32[128]{0:T(128)}, u32[]{:S(2)}) copy-start(f32[128]{0:T(128)} %get-tuple-element.130) | copy-start | bytes 1540
  58.5 2.5 %copy-start.80 = (f32[128]{0:T(128)S(1)}, f32[128]{0:T(128)}, u32[]{:S(2)}) copy-start(f32[128]{0:T(128)} %get-tuple-element.131) | copy-start | bytes 1540
  58.5 2.5 %copy-start.81 = (f32[128]{0:T(128)S(1)}, f32[128]{0:T(128)}, u32[]{:S(2)}) copy-start(f32[128]{0:T(128)} %get-tuple-element.132) | copy-start | bytes 1540
  58.5 2.5 %copy-start.36 = (f32[128]{0:T(128)S(1)}, f32[128]{0:T(128)}, u32[]{:S(2)}) copy-start(f32[128]{0:T(128)} %copy-done.35) | copy-start | bytes 1540
  58.5 2.5 %copy-start.38 = (f32[128]{0:T(128)S(1)}, f32[128]{0:T(128)}, u32[]{:S(2)}) copy-start(f32[128]{0:T(128)} %copy-done.37) | copy-start | bytes 1540
  58.5 2.5 %copy-start.40 = (f32[128]{0:T(128)S(1)}, f32[128]{0:T(128)}, u32[]{:S(2)}) copy-start(f32[128]{0:T(128)} %copy-done.39) | copy-start | bytes 1540
  58.5 2.5 %copy-start.76 = (f32[128]{0:T(128)S(1)}, f32[128]{0:T(128)}, u32[]{:S(2)}) copy-start(f32[128]{0:T(128)} %get-tuple-element.127) | copy-start | bytes 1540
  58.5 2.5 %copy-start.77 = (f32[128]{0:T(128)S(1)}, f32[128]{0:T(128)}, u32[]{:S(2)}) copy-start(f32[128]{0:T(128)} %get-tuple-element.128) | copy-start | bytes 1540
  58.5 2.5 %copy-start.78 = (f32[128]{0:T(128)S(1)}, f32[128]{0:T(128)}, u32[]{:S(2)}) copy-start(f32[128]{0:T(128)} %get-tuple-element.129) | copy-start | bytes 1540
  (68 other events, 77.1 us)
Sparse Core Ops, SparseCore 0:
  77.6 61.8 reduce-scatter.1
where the time goes:
time: 150 us; the launch traced here: 149 us
  waiting for transfers between devices  62 us (41%)
  other arithmetic  26.8 us (18%)
  local copies, waits for them, and re-layouts  24.7 us (16%)
  between operations  18.2 us (12%)
  matrix products  9.87 us (7%)
  starting transfers between devices  5.13 us (3%)
  blocking collectives  2.09 us (1%)
    reduce_scatter x1, waiting for transfers between devices, body(): lax.psum_scatter(partial_value, 'space', scatter_dimension=4, tiled=True)  62 us
    concatenate x8, other arithmetic, plane_roll(): gridded = jnp.roll(gridded, offset, axis=-2 if along_y else -1)  5.64 us
    ppermute x2, starting transfers between devices, passed_along(): return lax.ppermute(value, axis, pairs)  5.13 us
    reshape x8, local copies, waits for them, and re-layouts, plane_roll(): return gridded.reshape(initial)  4.68 us
    sub x12, other arithmetic, spin_apply(): summed_real = summed_real + coef_real * part_real - coef_imag * part_imag  4.45 us
    sub x15, other arithmetic, color_apply(): summed_real = summed_real + coef_real * part_real - coef_imag * part_imag  4.37 us
    slice x10, local copies, waits for them, and re-layouts, plane_roll(): gridded = jnp.roll(gridded, offset, axis=-2 if along_y else -1)  4.34 us
    sin x3, other arithmetic, contract(): sine_part = jnp.sin(theta)  4.05 us
  transfers between devices with their start and end apart: 3, of which 1 were waited for; matrix products, arithmetic and copies ran while one was open for 29% of the time, Pallas kernels for 0%

commit v1 on v0

v1 whole, which is shorter than its diff:
```python
import functools
import math

import jax
import jax.numpy as jnp
import numpy as np
from jax import lax
from jax.experimental import pallas as pl
from jax.experimental.pallas import tpu as pltpu
from jax.sharding import PartitionSpec as P

LX = 32
GROUP = 16


def gamma_tables():
    zeros = np.zeros((4, 4))
    gx_imag = np.array([[0, 0, 0, 1], [0, 0, 1, 0], [0, -1, 0, 0], [-1, 0, 0, 0]]) * 1.0
    gy_real = np.array([[0, 0, 0, -1], [0, 0, 1, 0], [0, 1, 0, 0], [-1, 0, 0, 0]]) * 1.0
    gz_imag = np.array([[0, 0, 1, 0], [0, 0, 0, -1], [-1, 0, 0, 0], [0, 1, 0, 0]]) * 1.0
    gt_real = np.array([[0, 0, 1, 0], [0, 0, 0, 1], [1, 0, 0, 0], [0, 1, 0, 0]]) * 1.0
    singles = [zeros + 1j * gx_imag, gy_real + 0j, 1j * gz_imag, gt_real + 0j]
    basis = []
    for number in range(16):
        matrix = np.eye(4) + 0j
        for which in range(4):
            if number >> which & 1:
                matrix = matrix @ singles[which]
        basis.append(matrix)
    return singles, np.stack(basis)


def unit_times(unit, value):
    real, imag = value
    if unit == 1:
        return real, imag
    if unit == -1:
        return -real, -imag
    if unit == 1j:
        return -imag, real
    return imag, -real


def small_times(matrix, half):
    outs = []
    for row in range(2):
        column = int(np.flatnonzero(matrix[row])[0])
        outs.append([unit_times(complex(matrix[row, column]), value) for value in half[column]])
    return outs


def added(first, second):
    return [
        [(a[0] + b[0], a[1] + b[1]) for a, b in zip(left, right)]
        for left, right in zip(first, second)
    ]


def subtracted(first, second):
    return [
        [(a[0] - b[0], a[1] - b[1]) for a, b in zip(left, right)]
        for left, right in zip(first, second)
    ]


def kernel(
    spaces,
    width_x,
    full_z,
    scaling,
    back_ref,
    fwd_ref,
    link_ref,
    momenta_ref,
    gamma_ref,
    table_ref,
    out_ref,
    other_back,
    links,
    halo_send,
    halo_recv,
    rows_scr,
    weave,
    weave_mm,
    pair,
    chunk_send,
    chunk_recv,
    back_sems,
    halo_send_sems,
    halo_recv_sems,
    chunk_send_sems,
    chunk_recv_sems,
):
    columns = fwd_ref.shape[3]
    plane = fwd_ref.shape[4]
    moments = momenta_ref.shape[0]
    here = lax.axis_index("space")
    core = lax.axis_index("spin")
    after = lax.rem(here + 1, spaces)
    before = lax.rem(here + spaces - 1, spaces)
    singles, _ = gamma_tables()

    barrier = pltpu.get_barrier_semaphore()
    pl.semaphore_signal(barrier, inc=1, device_id={"spin": 1 - core})
    for step in range(1, spaces):
        pl.semaphore_signal(
            barrier, inc=1, device_id={"space": lax.rem(here + step, spaces)}
        )

    for mu in range(3):
        for c in range(3):
            for d in range(3):
                row = ((mu * 3 + c) * 3 + d) * 2
                links[row : row + 2, :] = link_ref[mu, c, d].astype(jnp.float32)

    def link(mu, c, d):
        row = ((mu * 3 + c) * 3 + d) * 2
        return [
            jnp.broadcast_to(links[row + part : row + part + 1, :], (GROUP, plane))
            for part in range(2)
        ]

    def colour(mu, half, dagger):
        outs = [[None] * 3 for _ in range(2)]
        for c in range(3):
            for d in range(3):
                u_real, u_imag = link(mu, d, c) if dagger else link(mu, c, d)
                for spin in range(2):
                    v_real, v_imag = half[spin][d]
                    if dagger:
                        real = u_real * v_real + u_imag * v_imag
                        imag = u_real * v_imag - u_imag * v_real
                    else:
                        real = u_real * v_real - u_imag * v_imag
                        imag = u_real * v_imag + u_imag * v_real
                    held = outs[spin][c]
                    outs[spin][c] = (
                        (real, imag) if held is None else (held[0] + real, held[1] + imag)
                    )
        return outs

    lanes = lax.broadcasted_iota(jnp.int32, (GROUP, plane), 1)
    column_x = lax.rem(lanes, width_x)

    def rolled(value, steps, along_y):
        if along_y:
            return pltpu.roll(value, (steps * width_x) % plane, 1)
        plain = pltpu.roll(value, steps % plane, 1)
        wrapped = pltpu.roll(value, (steps - steps * width_x) % plane, 1)
        edge = 0 if steps == 1 else width_x - 1
        return jnp.where(column_x == edge, wrapped, plain)

    def rolled_half(half, steps, along_y):
        return [
            [tuple(rolled(part, steps, along_y) for part in value) for value in spin]
            for spin in half
        ]

    def spinor(cols):
        return [
            [
                tuple(fwd_ref[part, s, c, cols, :].astype(jnp.float32) for part in range(2))
                for c in range(3)
            ]
            for s in range(4)
        ]

    def group(index):
        return pl.ds(pl.multiple_of(index * GROUP, GROUP), GROUP)

    def halo_group(index, carry):
        cols = group(index)
        psi = spinor(cols)
        turned = small_times(singles[2][:2, 2:], psi[2:])
        minus = subtracted(psi[:2], turned)
        plus = colour(2, added(psi[:2], turned), True)
        for side, half in enumerate((minus, plus)):
            for spin in range(2):
                for c in range(3):
                    for part in range(2):
                        halo_send[side, part, spin, c, cols, :] = half[spin][c][part].astype(
                            jnp.bfloat16
                        )
        return carry

    lax.fori_loop(0, columns // GROUP, halo_group, 0)

    pl.semaphore_wait(barrier, spaces)

    halo_copies = []
    for side, target in ((0, before), (1, after)):
        copy = pltpu.make_async_remote_copy(
            src_ref=halo_send.at[side],
            dst_ref=halo_recv.at[side],
            send_sem=halo_send_sems.at[side],
            recv_sem=halo_recv_sems.at[side],
            device_id={"space": target},
        )
        copy.start()
        halo_copies.append(copy)
    back_copy = pltpu.make_async_remote_copy(
        src_ref=back_ref,
        dst_ref=other_back,
        send_sem=back_sems.at[0],
        recv_sem=back_sems.at[1],
        device_id={"spin": 1 - core},
    )
    back_copy.start()

    def store_weave(cols, full, first):
        for s in range(4):
            for c in range(3):
                for part in range(2):
                    value = full[s][c][part]
                    if not first:
                        value = value + weave[part, s, c, cols, :]
                    weave[part, s, c, cols, :] = value

    def plane_group(index, carry):
        cols = group(index)
        psi = spinor(cols)
        upper = lower = None
        for mu in range(2):
            turned = small_times(singles[mu][:2, 2:], psi[2:])
            ahead = colour(mu, rolled_half(subtracted(psi[:2], turned), -1, mu == 1), False)
            behind = rolled_half(colour(mu, added(psi[:2], turned), True), 1, mu == 1)
            up = subtracted(ahead, behind)
            low = small_times(-singles[mu][2:, :2], added(ahead, behind))
            upper = up if upper is None else added(upper, up)
            lower = low if lower is None else added(lower, low)
        store_weave(cols, upper + lower, True)
        return carry

    lax.fori_loop(0, columns // GROUP, plane_group, 0)

    sites = lax.broadcasted_iota(jnp.int32, (8, plane), 1)
    coord_x = lax.rem(sites, width_x).astype(jnp.float32)
    coord_y = lax.div(sites, width_x).astype(jnp.float32)
    coord_z = here.astype(jnp.float32)
    phases = []
    for number in range(moments):
        momentum = [momenta_ref[number, axis].astype(jnp.float32) for axis in range(3)]
        turns = coord_x * (momentum[0] * (1.0 / width_x))
        turns = turns + coord_y * (momentum[1] * (width_x / plane))
        turns = turns + coord_z * (momentum[2] * (1.0 / full_z))
        theta = (2.0 * math.pi) * (turns - jnp.floor(turns))
        phases.append((jnp.cos(theta)[:1, :], jnp.sin(theta)[:1, :]))

    def arrange(half, source):
        rows = columns * 2 // spaces
        local = columns // rows
        for part in range(2):
            for c in range(3):
                lane = (part * 3 + c) * plane
                for s in range(4):
                    for j in range(local):
                        row = half * 4 * columns + (j * 4 + s) * rows
                        rows_scr[row : row + rows, lane : lane + plane] = source[
                            part, s, c, j * rows : (j + 1) * rows, :
                        ]

    arrange(0, back_ref)

    back_copy.wait_recv()
    arrange(1, other_back)

    for copy in halo_copies:
        copy.wait_recv()

    def depth_group(index, carry):
        cols = group(index)
        received = [
            [
                [
                    tuple(
                        halo_recv[side, part, spin, c, cols, :].astype(jnp.float32)
                        for part in range(2)
                    )
                    for c in range(3)
                ]
                for spin in range(2)
            ]
            for side in range(2)
        ]
        ahead = colour(2, received[0], False)
        behind = received[1]
        upper = subtracted(ahead, behind)
        lower = small_times(-singles[2][2:, :2], added(ahead, behind))
        store_weave(cols, upper + lower, False)
        return carry

    lax.fori_loop(0, columns // GROUP, depth_group, 0)

    local_chunks = spaces // 2
    chunk_rows = 4 * columns // local_chunks
    copies = {}
    for number in range(moments):
        cosine, sine = phases[number]
        for s in range(4):
            for c in range(3):
                real = weave[0, s, c]
                imag = weave[1, s, c]
                turned_real = (cosine * real + sine * imag).astype(jnp.bfloat16)
                turned_imag = (cosine * imag - sine * real).astype(jnp.bfloat16)
                rows_at = slice(s * columns, (s + 1) * columns)
                rows_next = slice((4 + s) * columns, (5 + s) * columns)
                lanes_at = slice(c * plane, (c + 1) * plane)
                lanes_next = slice((3 + c) * plane, (4 + c) * plane)
                weave_mm[number, rows_at, lanes_at] = turned_real
                weave_mm[number, rows_at, lanes_next] = turned_imag
                weave_mm[number, rows_next, lanes_at] = turned_imag
                weave_mm[number, rows_next, lanes_next] = -turned_real
        product = lax.dot_general(
            rows_scr[...],
            weave_mm[number],
            (((1,), (1,)), ((), ())),
            preferred_element_type=jnp.float32,
        )
        for half in range(2):
            owner = core if half == 0 else 1 - core
            for j in range(local_chunks):
                target = owner * local_chunks + j
                top = (half * local_chunks + j) * chunk_rows
                for part in range(2):
                    piece = product[
                        top : top + chunk_rows, part * 4 * columns : (part + 1) * 4 * columns
                    ]
                    pair[number, target, part] = piece
                    chunk_send[number, target, part] = piece.astype(jnp.bfloat16)

        if number > 0:
            send_chunks(number - 1, spaces, here, chunk_send, chunk_recv, chunk_send_sems,
                        chunk_recv_sems, copies)
    tables = [table_ref[gamma_ref[k]] for k in range(gamma_ref.shape[0])]
    send_chunks(moments - 1, spaces, here, chunk_send, chunk_recv, chunk_send_sems,
                chunk_recv_sems, copies)

    rows = chunk_rows // 4
    for number in range(moments):
        total = [pair[number, here, part] for part in range(2)]
        for step in range(1, spaces):
            copies[number, step].wait_recv()
            for part in range(2):
                total[part] = total[part] + chunk_recv[number, step - 1, part].astype(
                    jnp.float32
                )
        total = [value * scaling for value in total]
        spins = [
            [value[s * rows : (s + 1) * rows, :] for s in range(4)] for value in total
        ]
        for k in range(gamma_ref.shape[0]):
            real = imag = None
            for s in range(4):
                g_real = tables[k][s : s + 1, :]
                g_imag = tables[k][4 + s : 5 + s, :]
                one = g_real * spins[0][s] - g_imag * spins[1][s]
                two = g_real * spins[1][s] + g_imag * spins[0][s]
                real = one if real is None else real + one
                imag = two if imag is None else imag + two
            for part, value in enumerate((real, imag)):
                summed = value[:, :columns]
                for other in range(1, 4):
                    summed = summed + value[:, other * columns : (other + 1) * columns]
                out_ref[part, number, k] = summed

    back_copy.wait_send()
    for copy in halo_copies:
        copy.wait_send()
    for copy in copies.values():
        copy.wait_send()


def send_chunks(
    number, spaces, here, chunk_send, chunk_recv, chunk_send_sems, chunk_recv_sems, copies
):
    for step in range(1, spaces):
        target = lax.rem(here + step, spaces)
        copy = pltpu.make_async_remote_copy(
            src_ref=chunk_send.at[number, target],
            dst_ref=chunk_recv.at[number, step - 1],
            send_sem=chunk_send_sems.at[number, step - 1],
            recv_sem=chunk_recv_sems.at[number, step - 1],
            device_id={"space": target},
        )
        copy.start()
        copies[number, step] = copy


def body(mesh, backward, forward, gauge_links, momenta, gamma_list):
    spaces = mesh.shape["space"]
    _, times, _, columns, _, layers, plane = forward.shape
    moments = momenta.shape[0]
    gammas = gamma_list.shape[0]
    rows = columns * mesh.shape["spin"] // spaces
    back = jnp.transpose(backward, (0, 1, 2, 4, 5, 3, 6)).reshape(2, 4, 3, columns, plane)
    fwd = jnp.transpose(forward, (0, 1, 2, 4, 5, 3, 6)).reshape(2, 4, 3, columns, plane)
    link = jnp.transpose(gauge_links, (1, 2, 3, 4, 5, 0, 6)).reshape(3, 3, 3, 2, plane)
    full_z = layers * spaces
    scaling = 0.5 / math.sqrt(3.0 * plane * full_z)
    _, basis = gamma_tables()
    table = np.concatenate([basis.real, basis.imag], axis=1)
    table = np.repeat(table, columns, axis=2).astype(np.float32)
    vmem = pl.BlockSpec(memory_space=pltpu.VMEM)
    smem = pl.BlockSpec(memory_space=pltpu.SMEM)
    out = pl.pallas_call(
        functools.partial(kernel, spaces, LX, full_z, scaling),
        out_shape=jax.ShapeDtypeStruct((2, moments, gammas, rows, columns), jnp.float32),
        in_specs=[vmem, vmem, vmem, smem, smem, vmem],
        out_specs=vmem,
        scratch_shapes=[
            pltpu.VMEM((2, 4, 3, columns, plane), jnp.bfloat16),
            pltpu.VMEM((56, plane), jnp.float32),
            pltpu.VMEM((2, 2, 2, 3, columns, plane), jnp.bfloat16),
            pltpu.VMEM((2, 2, 2, 3, columns, plane), jnp.bfloat16),
            pltpu.VMEM((8 * columns, 6 * plane), jnp.bfloat16),
            pltpu.VMEM((2, 4, 3, columns, plane), jnp.float32),
            pltpu.VMEM((moments, 8 * columns, 6 * plane), jnp.bfloat16),
            pltpu.VMEM((moments, spaces, 2, 4 * rows, 4 * columns), jnp.float32),
            pltpu.VMEM((moments, spaces, 2, 4 * rows, 4 * columns), jnp.bfloat16),
            pltpu.VMEM((moments, spaces - 1, 2, 4 * rows, 4 * columns), jnp.bfloat16),
            pltpu.SemaphoreType.DMA((2,)),
            pltpu.SemaphoreType.DMA((2,)),
            pltpu.SemaphoreType.DMA((2,)),
            pltpu.SemaphoreType.DMA((moments, spaces - 1)),
            pltpu.SemaphoreType.DMA((moments, spaces - 1)),
        ],
        compiler_params=pltpu.CompilerParams(collective_id=0, has_side_effects=True),
    )(back, fwd, link, momenta, gamma_list, table)
    return out.reshape(2, moments, gammas, times, rows, columns)


def solution(mesh):
    in_specs = (
        P("parts", "tm", None, "spin", None, "space", None),
        P("parts", "tm", None, "spin", None, "space", None),
        P("parts", None, None, None, "tm", "space", None),
        P(),
        P(),
    )
    out_specs = P("parts", None, None, "tm", "space", "spin")
    return jax.shard_map(
        functools.partial(body, mesh),
        mesh=mesh,
        in_specs=in_specs,
        out_specs=out_specs,
        check_vma=False,
    )
```

time: 150 us -> 24.3 us (0.16)
  waiting for transfers between devices: 62 us -> 0 us
  other arithmetic: 26.8 us -> 0 us
  local copies, waits for them, and re-layouts: 24.7 us -> 2.1 us
  Pallas kernels: 0 us -> 22 us
  between operations: 18.2 us -> 0.01 us
  matrix products: 9.87 us -> 0 us
  starting transfers between devices: 5.13 us -> 0 us
  blocking collectives: 2.09 us -> 0 us
    reduce_scatter x1 -> x0, waiting for transfers between devices: 62 us -> none  [body(): lax.psum_scatter(partial_value, 'space', scatter_dimension=4, tiled=True)]
    pallas_call x0 -> x1, Pallas kernels: none -> 22 us  [body(): pl.pallas_call(functools.partial(kernel, spaces, LX, full_z, scaling), ou...]
    dot_general x18 -> x0, matrix products: 9.5 us -> none  [the longest x3 1.88 us: contract(): jnp.einsum('ksv,usvab->kuab', gam_imag, pair_imag, precision=lax.Precisio...]
    sub x27 -> x0, other arithmetic: 8.82 us -> none  [the longest x12 4.45 us: spin_apply(): summed_real = summed_real + coef_real * part_real - coef_imag * part_imag]
    another operation x61 -> x0, local copies, waits for them, and re-layouts: 6.16 us -> none  [the longest x1 2.8 us: contract(): return jnp.stack(blocks, axis=1)]
    concatenate x8 -> x0, other arithmetic: 5.64 us -> none  [plane_roll(): gridded = jnp.roll(gridded, offset, axis=-2 if along_y else -1)]
    ppermute x2 -> x0, starting transfers between devices: 5.13 us -> none  [passed_along(): return lax.ppermute(value, axis, pairs)]
    slice x11 -> x0, local copies, waits for them, and re-layouts: 5.02 us -> none  [the longest x10 4.34 us: plane_roll(): gridded = jnp.roll(gridded, offset, axis=-2 if along_y else -1)]
  transfers between devices with their start and end apart: 3 -> 0, of which waited for: 1 -> 0; matrix products, arithmetic and copies ran while one was open for 29% -> 0% of each run, Pallas kernels for 0% -> 0%
where the time goes in v1:
time: 24.3 us; the launch traced here: 24.1 us
  Pallas kernels  22 us (91%)
  local copies, waits for them, and re-layouts  2.1 us (9%)
    pallas_call x1, Pallas kernels, body(): pl.pallas_call(functools.partial(kernel, spaces, LX, full_z, scaling), ou...  22 us
    unnamed x1, local copies, waits for them, and re-layouts  2.1 us

profile of v1, /device:TPU:0, one launch (start us, length us, event | category | flops | bytes accessed | tf_op | source)
XLA Modules:
  0.0 24.1 jit_solution(3804343714627160041)
XLA Ops:
  0.0 22.0 %shard_map.64 = f32[2,3,16,16,32]{4,3,2,1,0:T(8,128)} custom-call(bf16[2,4,3,32,128]{4,3,2,1,0:T(8,128)(2,1)} %bitcast.19, bf16[2,4,3,32,128]{4,3,2,1,0:T(8,128)(2,1)} %bitcast.20, bf16[3,3,3,2,128]{4,3,2,1,0:T(2,128)(2,1)} %bitcast.21, s32[3,3]{1,0:T(4,128)} %momenta_ref.1, s32[16]{0:T(128)} %gamma_ref.1, f32[16,8,128]{2,1,0:T(8,128)} %constant.2.clone.table_ref), custom_call_target="tpu_custom_call" | custom-call | tf_op jit(solution)/shard_map/pallas_call | solution.py:405
  22.0 2.1 %copy.12 = f32[2,3,16,1,16,32]{5,4,3,2,1,0:T(8,128)} copy(f32[2,3,16,1,16,32]{5,4,3,2,1,0:T(8,128)} %bitcast.18) | data formatting | bytes 393216

commit v2 on v1

--- a/solution.py
+++ b/solution.py
@@ -68,13 +68,17 @@
     width_x,
     full_z,
     scaling,
-    back_ref,
-    fwd_ref,
-    link_ref,
+    back_hbm,
+    fwd_hbm,
+    link_hbm,
     momenta_ref,
     gamma_ref,
     table_ref,
     out_ref,
+    chosen_ref,
+    back_ref,
+    fwd_ref,
+    link_ref,
     other_back,
     links,
     halo_send,
@@ -85,12 +89,21 @@
     pair,
     chunk_send,
     chunk_recv,
+    load_sems,
     back_sems,
     halo_send_sems,
     halo_recv_sems,
     chunk_send_sems,
     chunk_recv_sems,
 ):
+    loads = [
+        pltpu.make_async_copy(source, target, load_sems.at[number])
+        for number, (source, target) in enumerate(
+            ((fwd_hbm, fwd_ref), (link_hbm, link_ref), (back_hbm, back_ref))
+        )
+    ]
+    for load in loads:
+        load.start()
     columns = fwd_ref.shape[3]
     plane = fwd_ref.shape[4]
     moments = momenta_ref.shape[0]
@@ -107,6 +120,8 @@
             barrier, inc=1, device_id={"space": lax.rem(here + step, spaces)}
         )
 
+    for load in loads[:2]:
+        load.wait()
     for mu in range(3):
         for c in range(3):
             for d in range(3):
@@ -198,6 +213,7 @@
         )
         copy.start()
         halo_copies.append(copy)
+    loads[2].wait()
     back_copy = pltpu.make_async_remote_copy(
         src_ref=back_ref,
         dst_ref=other_back,
@@ -331,11 +347,11 @@
         if number > 0:
             send_chunks(number - 1, spaces, here, chunk_send, chunk_recv, chunk_send_sems,
                         chunk_recv_sems, copies)
-    tables = [table_ref[gamma_ref[k]] for k in range(gamma_ref.shape[0])]
+    for k in range(gamma_ref.shape[0]):
+        chosen_ref[k] = table_ref[gamma_ref[k]]
     send_chunks(moments - 1, spaces, here, chunk_send, chunk_recv, chunk_send_sems,
                 chunk_recv_sems, copies)
 
-    rows = chunk_rows // 4
     for number in range(moments):
         total = [pair[number, here, part] for part in range(2)]
         for step in range(1, spaces):
@@ -344,15 +360,29 @@
                 total[part] = total[part] + chunk_recv[number, step - 1, part].astype(
                     jnp.float32
                 )
-        total = [value * scaling for value in total]
+        for part in range(2):
+            out_ref[number, part] = total[part] * scaling
+
+    back_copy.wait_send()
+    for copy in halo_copies:
+        copy.wait_send()
+    for copy in copies.values():
+        copy.wait_send()
+
+
+def insert_kernel(chosen_ref, pair_ref, out_hbm, out_ref, sems):
+    moments, gammas, rows, columns = out_ref.shape[1:]
+    stores = []
+    for number in range(moments):
         spins = [
-            [value[s * rows : (s + 1) * rows, :] for s in range(4)] for value in total
+            [pair_ref[number, part, s * rows : (s + 1) * rows, :] for s in range(4)]
+            for part in range(2)
         ]
-        for k in range(gamma_ref.shape[0]):
+        for k in range(gammas):
             real = imag = None
             for s in range(4):
-                g_real = tables[k][s : s + 1, :]
-                g_imag = tables[k][4 + s : 5 + s, :]
+                g_real = chosen_ref[k, s : s + 1, :]
+                g_imag = chosen_ref[k, 4 + s : 5 + s, :]
                 one = g_real * spins[0][s] - g_imag * spins[1][s]
                 two = g_real * spins[1][s] + g_imag * spins[0][s]
                 real = one if real is None else real + one
@@ -362,12 +392,14 @@
                 for other in range(1, 4):
                     summed = summed + value[:, other * columns : (other + 1) * columns]
                 out_ref[part, number, k] = summed
-
-    back_copy.wait_send()
-    for copy in halo_copies:
-        copy.wait_send()
-    for copy in copies.values():
-        copy.wait_send()
+        stores.append(
+            pltpu.make_async_copy(out_ref.at[:, number], out_hbm.at[:, number], sems.at[number])
+        )
+        if number > 0:
+            stores[number - 1].start()
+    stores[-1].start()
+    for store in stores:
+        store.wait()
 
 
 def send_chunks(
@@ -401,13 +433,20 @@
     table = np.concatenate([basis.real, basis.imag], axis=1)
     table = np.repeat(table, columns, axis=2).astype(np.float32)
     vmem = pl.BlockSpec(memory_space=pltpu.VMEM)
+    anywhere = pl.BlockSpec(memory_space=pl.ANY)
     smem = pl.BlockSpec(memory_space=pltpu.SMEM)
-    out = pl.pallas_call(
+    pairs, chosen = pl.pallas_call(
         functools.partial(kernel, spaces, LX, full_z, scaling),
-        out_shape=jax.ShapeDtypeStruct((2, moments, gammas, rows, columns), jnp.float32),
-        in_specs=[vmem, vmem, vmem, smem, smem, vmem],
-        out_specs=vmem,
+        out_shape=[
+            pltpu.VMEM((moments, 2, 4 * rows, 4 * columns), jnp.float32),
+            pltpu.VMEM((gammas,) + table.shape[1:], jnp.float32),
+        ],
+        in_specs=[anywhere, anywhere, anywhere, smem, smem, vmem],
+        out_specs=[vmem, vmem],
         scratch_shapes=[
+            pltpu.VMEM(back.shape, back.dtype),
+            pltpu.VMEM(fwd.shape, fwd.dtype),
+            pltpu.VMEM(link.shape, link.dtype),
             pltpu.VMEM((2, 4, 3, columns, plane), jnp.bfloat16),
             pltpu.VMEM((56, plane), jnp.float32),
             pltpu.VMEM((2, 2, 2, 3, columns, plane), jnp.bfloat16),
@@ -418,6 +457,7 @@
             pltpu.VMEM((moments, spaces, 2, 4 * rows, 4 * columns), jnp.float32),
             pltpu.VMEM((moments, spaces, 2, 4 * rows, 4 * columns), jnp.bfloat16),
             pltpu.VMEM((moments, spaces - 1, 2, 4 * rows, 4 * columns), jnp.bfloat16),
+            pltpu.SemaphoreType.DMA((3,)),
             pltpu.SemaphoreType.DMA((2,)),
             pltpu.SemaphoreType.DMA((2,)),
             pltpu.SemaphoreType.DMA((2,)),
@@ -426,6 +466,20 @@
         ],
         compiler_params=pltpu.CompilerParams(collective_id=0, has_side_effects=True),
     )(back, fwd, link, momenta, gamma_list, table)
+    out_shape = (2, moments, gammas, rows, columns)
+    out = pl.pallas_call(
+        insert_kernel,
+        out_shape=jax.ShapeDtypeStruct(out_shape, jnp.float32),
+        in_specs=[vmem, vmem],
+        out_specs=anywhere,
+        scratch_shapes=[
+            pltpu.VMEM(out_shape, jnp.float32),
+            pltpu.SemaphoreType.DMA((moments,)),
+        ],
+    )(
+        pltpu.with_memory_space_constraint(chosen, pltpu.VMEM),
+        pltpu.with_memory_space_constraint(pairs, pltpu.VMEM),
+    )
     return out.reshape(2, moments, gammas, times, rows, columns)
 
 

time: 24.3 us -> 22.4 us (0.922)
  local copies, waits for them, and re-layouts: 2.1 us -> 0 us
    unnamed x1 -> x0, local copies, waits for them, and re-layouts: 2.1 us -> none
    pallas_call x0 -> x1, Pallas kernels: none -> 1.5 us  [body(): pl.pallas_call(insert_kernel, out_shape=jax.ShapeDtypeStruct(out_shape, j...]
    pallas_call x1, Pallas kernels: 22 us -> 20.7 us  [body(): pl.pallas_call(functools.partial(kernel, spaces, LX, full_z, scaling), ou...]
where the time goes in v2:
time: 22.4 us; the launch traced here: 22.2 us
  Pallas kernels  22.2 us (99%)
    pallas_call x1, Pallas kernels, body(): pl.pallas_call(functools.partial(kernel, spaces, LX, full_z, scaling), ou...  20.7 us
    pallas_call x1, Pallas kernels, body(): pl.pallas_call(insert_kernel, out_shape=jax.ShapeDtypeStruct(out_shape, j...  1.5 us

profile of v2, /device:TPU:0, one launch (start us, length us, event | category | flops | bytes accessed | tf_op | source)
XLA Modules:
  0.0 22.2 jit_solution(3084254045836554905)
XLA Ops:
  0.0 20.7 %shard_map.64 = (f32[3,2,64,128]{3,2,1,0:T(8,128)S(1)}, f32[16,8,128]{2,1,0:T(8,128)S(1)}) custom-call(bf16[2,4,3,32,128]{4,3,2,1,0:T(8,128)(2,1)} %bitcast.18, bf16[2,4,3,32,128]{4,3,2,1,0:T(8,128)(2,1)} %bitcast.19, bf16[3,3,3,2,128]{4,3,2,1,0:T(2,128)(2,1)} %bitcast.20, s32[3,3]{1,0:T(4,128)} %momenta_ref.1, s32[16]{0:T(128)} %gamma_ref.1, ...), custom_call_target="tpu_custom_call" | custom-call | tf_op jit(solution)/shard_map/pallas_call | solution.py:438
  20.7 1.5 %shard_map.65 = f32[2,3,16,16,32]{4,3,2,1,0:T(8,128)} custom-call(f32[16,8,128]{2,1,0:T(8,128)S(1)} %get-tuple-element.7.chosen_ref, f32[3,2,64,128]{3,2,1,0:T(8,128)S(1)} %get-tuple-element.8.pair_ref), custom_call_target="tpu_custom_call" | custom-call | tf_op jit(solution)/shard_map/pallas_call | solution.py:470

commit v3 on v2

--- a/solution.py
+++ b/solution.py
@@ -89,13 +89,17 @@
     pair,
     chunk_send,
     chunk_recv,
+    relay_recv,
     load_sems,
     back_sems,
     halo_send_sems,
     halo_recv_sems,
     chunk_send_sems,
     chunk_recv_sems,
+    relay_send_sems,
+    relay_recv_sems,
 ):
+    relay_sems = (relay_send_sems, relay_recv_sems)
     loads = [
         pltpu.make_async_copy(source, target, load_sems.at[number])
         for number, (source, target) in enumerate(
@@ -310,6 +314,7 @@
     local_chunks = spaces // 2
     chunk_rows = 4 * columns // local_chunks
     copies = {}
+    relays = {}
     for number in range(moments):
         cosine, sine = phases[number]
         for s in range(4):
@@ -346,27 +351,41 @@
 
         if number > 0:
             send_chunks(number - 1, spaces, here, chunk_send, chunk_recv, chunk_send_sems,
-                        chunk_recv_sems, copies)
+                        chunk_recv_sems, copies, relays, relay_recv, relay_sems)
+    send_chunks(moments - 1, spaces, here, chunk_send, chunk_recv, chunk_send_sems,
+                chunk_recv_sems, copies, relays, relay_recv, relay_sems)
+
+    late = None
+    for number in range(moments):
+        for part in sorted(relay_steps(spaces)):
+            relays[number, part].wait_recv()
+            step = relay_steps(spaces)[part]
+            target = lax.rem(here + step, spaces)
+            joined = pair[number, target, part] + relay_recv[number, part].astype(jnp.float32)
+            chunk_send[number, target, part] = joined.astype(jnp.bfloat16)
+            if late is not None:
+                send_piece(late, spaces, here, chunk_send, chunk_recv, chunk_send_sems,
+                           chunk_recv_sems, copies)
+            late = (number, step, part)
     for k in range(gamma_ref.shape[0]):
         chosen_ref[k] = table_ref[gamma_ref[k]]
-    send_chunks(moments - 1, spaces, here, chunk_send, chunk_recv, chunk_send_sems,
-                chunk_recv_sems, copies)
+    if late is not None:
+        send_piece(late, spaces, here, chunk_send, chunk_recv, chunk_send_sems,
+                   chunk_recv_sems, copies)
 
     for number in range(moments):
-        total = [pair[number, here, part] for part in range(2)]
-        for step in range(1, spaces):
-            copies[number, step].wait_recv()
-            for part in range(2):
-                total[part] = total[part] + chunk_recv[number, step - 1, part].astype(
-                    jnp.float32
-                )
         for part in range(2):
-            out_ref[number, part] = total[part] * scaling
+            total = pair[number, here, part]
+            for step in range(1, spaces):
+                if (number, step, part) in copies:
+                    copies[number, step, part].wait_recv()
+                    total = total + chunk_recv[number, step - 1, part].astype(jnp.float32)
+            out_ref[number, part] = total * scaling
 
     back_copy.wait_send()
     for copy in halo_copies:
         copy.wait_send()
-    for copy in copies.values():
+    for copy in (*copies.values(), *relays.values()):
         copy.wait_send()
 
 
@@ -402,20 +421,49 @@
         store.wait()
 
 
+def relay_steps(spaces):
+    half = spaces // 2
+    return {0: half - 1, 1: spaces - half + 1} if half > 1 else {}
+
+
+def send_piece(
+    piece, spaces, here, chunk_send, chunk_recv, chunk_send_sems, chunk_recv_sems, copies
+):
+    number, step, part = piece
+    target = lax.rem(here + step, spaces)
+    copy = pltpu.make_async_remote_copy(
+        src_ref=chunk_send.at[number, target, part],
+        dst_ref=chunk_recv.at[number, step - 1, part],
+        send_sem=chunk_send_sems.at[number, step - 1, part],
+        recv_sem=chunk_recv_sems.at[number, step - 1, part],
+        device_id={"space": target},
+    )
+    copy.start()
+    copies[piece] = copy
+
+
 def send_chunks(
-    number, spaces, here, chunk_send, chunk_recv, chunk_send_sems, chunk_recv_sems, copies
+    number, spaces, here, chunk_send, chunk_recv, chunk_send_sems, chunk_recv_sems, copies,
+    relays, relay_recv, relay_sems,
 ):
-    for step in range(1, spaces):
-        target = lax.rem(here + step, spaces)
+    half = spaces // 2
+    merged = relay_steps(spaces)
+    for part in merged:
         copy = pltpu.make_async_remote_copy(
-            src_ref=chunk_send.at[number, target],
-            dst_ref=chunk_recv.at[number, step - 1],
-            send_sem=chunk_send_sems.at[number, step - 1],
-            recv_sem=chunk_recv_sems.at[number, step - 1],
-            device_id={"space": target},
+            src_ref=chunk_send.at[number, lax.rem(here + half, spaces), part],
+            dst_ref=relay_recv.at[number, part],
+            send_sem=relay_sems[0].at[number, part],
+            recv_sem=relay_sems[1].at[number, part],
+            device_id={"space": lax.rem(here + (1 if part == 0 else spaces - 1), spaces)},
         )
         copy.start()
-        copies[number, step] = copy
+        relays[number, part] = copy
+    for step in range(1, spaces):
+        for part in range(2):
+            if merged and (step == half or merged[part] == step):
+                continue
+            send_piece((number, step, part), spaces, here, chunk_send, chunk_recv,
+                       chunk_send_sems, chunk_recv_sems, copies)
 
 
 def body(mesh, backward, forward, gauge_links, momenta, gamma_list):
@@ -457,12 +505,15 @@
             pltpu.VMEM((moments, spaces, 2, 4 * rows, 4 * columns), jnp.float32),
             pltpu.VMEM((moments, spaces, 2, 4 * rows, 4 * columns), jnp.bfloat16),
             pltpu.VMEM((moments, spaces - 1, 2, 4 * rows, 4 * columns), jnp.bfloat16),
+            pltpu.VMEM((moments, 2, 4 * rows, 4 * columns), jnp.bfloat16),
             pltpu.SemaphoreType.DMA((3,)),
             pltpu.SemaphoreType.DMA((2,)),
             pltpu.SemaphoreType.DMA((2,)),
             pltpu.SemaphoreType.DMA((2,)),
-            pltpu.SemaphoreType.DMA((moments, spaces - 1)),
-            pltpu.SemaphoreType.DMA((moments, spaces - 1)),
+            pltpu.SemaphoreType.DMA((moments, spaces - 1, 2)),
+            pltpu.SemaphoreType.DMA((moments, spaces - 1, 2)),
+            pltpu.SemaphoreType.DMA((moments, 2)),
+            pltpu.SemaphoreType.DMA((moments, 2)),
         ],
         compiler_params=pltpu.CompilerParams(collective_id=0, has_side_effects=True),
     )(back, fwd, link, momenta, gamma_list, table)

time: 22.4 us -> 25.3 us (1.13)
  Pallas kernels: 22.2 us -> 25.1 us
    pallas_call x1, Pallas kernels: 20.7 us -> 23.6 us  [body(): pl.pallas_call(functools.partial(kernel, spaces, LX, full_z, scaling), ou...]
where the time goes in v3:
time: 25.3 us; the launch traced here: 25.2 us
  Pallas kernels  25.1 us (99%)
    pallas_call x1, Pallas kernels, body(): pl.pallas_call(functools.partial(kernel, spaces, LX, full_z, scaling), ou...  23.6 us
    pallas_call x1, Pallas kernels, body(): pl.pallas_call(insert_kernel, out_shape=jax.ShapeDtypeStruct(out_shape, j...  1.5 us

profile of v3, /device:TPU:0, one launch (start us, length us, event | category | flops | bytes accessed | tf_op | source)
XLA Modules:
  0.0 25.2 jit_solution(9297197302313144992)
XLA Ops:
  0.0 23.6 %shard_map.64 = (f32[3,2,64,128]{3,2,1,0:T(8,128)S(1)}, f32[16,8,128]{2,1,0:T(8,128)S(1)}) custom-call(bf16[2,4,3,32,128]{4,3,2,1,0:T(8,128)(2,1)} %bitcast.18, bf16[2,4,3,32,128]{4,3,2,1,0:T(8,128)(2,1)} %bitcast.19, bf16[3,3,3,2,128]{4,3,2,1,0:T(2,128)(2,1)} %bitcast.20, s32[3,3]{1,0:T(4,128)} %momenta_ref.1, s32[16]{0:T(128)} %gamma_ref.1, ...), custom_call_target="tpu_custom_call" | custom-call | tf_op jit(solution)/shard_map/pallas_call | solution.py:486
  23.7 1.5 %shard_map.65 = f32[2,3,16,16,32]{4,3,2,1,0:T(8,128)} custom-call(f32[16,8,128]{2,1,0:T(8,128)S(1)} %get-tuple-element.7.chosen_ref, f32[3,2,64,128]{3,2,1,0:T(8,128)S(1)} %get-tuple-element.8.pair_ref), custom_call_target="tpu_custom_call" | custom-call | tf_op jit(solution)/shard_map/pallas_call | solution.py:521
